TPU v7x, 32 devices: a whole 2x2x4 slice. The times are simulated.
32 devices in a mesh: tm: 16 (over z, x, core), space: 2 (over y).
Axes of the slice: x: 2, y: 2, z: 4, core: 2. Of those that a mesh axis runs over, the one named last changes fastest.
Arguments:
- forcing: float32 [16, 8, 128, 128], P('tm', 'space'), may hold values from -6 to 6
- initial: float32 [8, 128, 128], P('space'), may hold values from -6 to 6
- coupling: float32 [8, 128, 128], P('space'), may hold values from 0.3 to 3
- velocity: float32 [3, 8, 128, 128], P(None, 'space'), may hold values from -0.9 to 0.9
Outputs:
- iterate: float32 [16, 8, 128, 128], P('tm', 'space')
All inputs are finite; a program needn't handle non-finite values.
Results may differ from a plain program's by a relative error of at most 0.0003.
Values sent between devices are 32-bit elements; how exact they have to be, the bound alone decides.
No kernel may reach another device: no remote copies, remote signals or barrier semaphores. Data moves between devices by JAX's collectives and lax.ppermute only.
A program may use at most 64 MiB of HBM per device.

v0:
```python
import math

import jax
import jax.numpy as jnp
from jax import lax
from jax.sharding import PartitionSpec as P

ITERS = 2
SWEEPS = 8


wrap_alpha = 0.1


def passed_along(array, axis, by):
    size = lax.axis_size(axis)
    pairs = [(i, i + by) for i in range(size) if 0 <= i + by < size]
    return lax.ppermute(array, axis, pairs)


def with_halo(block, sides, width):
    for axis, dim in sides:
        count = lax.axis_size(axis)
        forward = [(i, i + 1) for i in range(count - 1)]
        backward = [(target, source) for source, target in forward]
        low = lax.ppermute(
            lax.slice_in_dim(block, block.shape[dim] - width, None, axis=dim), axis, forward
        )
        high = lax.ppermute(lax.slice_in_dim(block, 0, width, axis=dim), axis, backward)
        block = jnp.concatenate([low, block, high], axis=dim)
    return block


def coupled(extended, coupling, advect):
    total = (coupling - advect[0]) * extended[..., 2:, 1:-1, 1:-1] + (
        coupling + advect[0]
    ) * extended[..., :-2, 1:-1, 1:-1]
    total = (
        total
        + (coupling - advect[1]) * extended[..., 1:-1, 2:, 1:-1]
        + (coupling + advect[1]) * extended[..., 1:-1, :-2, 1:-1]
    )
    total = (
        total
        + (coupling - advect[2]) * extended[..., 1:-1, 1:-1, 2:]
        + (coupling + advect[2]) * extended[..., 1:-1, 1:-1, :-2]
    )
    return total


def tables(total_steps):
    indices = jnp.arange(total_steps, dtype=jnp.int32)
    products = indices[:, None] * indices[None, :] % total_steps
    angles = products.astype(jnp.float32) * (2.0 * math.pi / total_steps)
    return (jnp.cos(angles), jnp.sin(angles))


def matmul(table, columns):
    return jnp.dot(
        table, columns, preferred_element_type=jnp.float32, precision=lax.Precision.HIGHEST
    )


def jacobi(spectrum, coupling, advect, frequency, total_steps, extend):
    radius = math.exp(math.log(wrap_alpha) / total_steps)
    angles = (frequency * (2.0 * math.pi / total_steps))[:, None, None, None]
    diag_re = 1.0 + 6.0 * coupling - radius * jnp.cos(angles)
    diag_im = radius * jnp.sin(angles) + jnp.zeros_like(diag_re)
    modulus = diag_re * diag_re + diag_im * diag_im
    source_re = spectrum[0]
    source_im = spectrum[1]
    value_re = (source_re * diag_re + source_im * diag_im) / modulus
    value_im = (source_im * diag_re - source_re * diag_im) / modulus
    for sweep in range(SWEEPS):
        extended = extend(jnp.stack([value_re, value_im]))
        summed = coupled(extended, coupling, advect)
        sum_re = source_re + summed[0]
        sum_im = source_im + summed[1]
        value_re = (sum_re * diag_re + sum_im * diag_im) / modulus
        value_im = (sum_im * diag_re - sum_re * diag_im) / modulus
    return jnp.stack([value_re, value_im])


def body(forcing, initial, coupling, velocity):
    local_steps = forcing.shape[0]
    groups = lax.axis_size("tm")
    total_steps = local_steps * groups
    time_index = lax.axis_index("tm")
    advect = coupling[None] * velocity
    cosine, sine_table = tables(total_steps)
    global_steps = (time_index * local_steps + jnp.arange(local_steps, dtype=jnp.int32)).astype(
        jnp.float32
    )
    time_weight = jnp.exp(math.log(wrap_alpha) * global_steps / total_steps)[:, None, None, None]
    iterate = jnp.broadcast_to(initial, forcing.shape)

    def forward(piece):
        columns = piece.reshape(piece.shape[0], -1)
        spec_re = matmul(cosine, columns)
        spec_im = -matmul(sine_table, columns)
        return jnp.stack([spec_re, spec_im]).reshape((2,) + piece.shape)

    for repeat in range(ITERS):
        before = passed_along(iterate[-1], "tm", 1)
        before = jnp.where(time_index == 0, initial, before)
        previous = jnp.concatenate([before[None], iterate[:-1]], axis=0)
        extended = with_halo(iterate, (("space", 1),), 1)
        extended = jnp.pad(extended, ((0, 0), (0, 0), (1, 1), (1, 1)))
        residual = (
            forcing
            - ((1.0 + 6.0 * coupling) * iterate - coupled(extended, coupling, advect))
            + previous
        )
        scaled = residual * time_weight
        spectrum = forward(lax.all_to_all(scaled, "tm", split_axis=2, concat_axis=0, tiled=True))
        blocked = lax.all_to_all(spectrum, "tm", split_axis=1, concat_axis=3, tiled=True)
        frequency = (time_index * local_steps + jnp.arange(local_steps, dtype=jnp.int32)).astype(
            jnp.float32
        )

        def extend_narrow(field):
            grown = with_halo(field, (("space", 2),), 1)
            return jnp.pad(grown, ((0, 0), (0, 0), (0, 0), (1, 1), (1, 1)))

        solved = jacobi(blocked, coupling, advect, frequency, total_steps, extend_narrow)
        spectrum_out = lax.all_to_all(solved, "tm", split_axis=3, concat_axis=1, tiled=True)
        inverse_part = (
            matmul(cosine, spectrum_out[0].reshape(total_steps, -1))
            - matmul(sine_table, spectrum_out[1].reshape(total_steps, -1))
        ) / total_steps
        inverse_part = inverse_part.reshape(spectrum_out.shape[1:])
        correction = lax.all_to_all(inverse_part, "tm", split_axis=0, concat_axis=2, tiled=True)
        iterate = iterate + correction / time_weight
    return iterate


def solution(mesh):
    return jax.shard_map(
        body,
        mesh=mesh,
        in_specs=(
            P("tm", "space", None, None),
            P("space", None, None),
            P("space", None, None),
            P(None, "space", None, None),
        ),
        out_specs=P("tm", "space", None, None),
        check_vma=False,
    )
```

profile of v0, /device:TPU:0, one launch (start us, length us, event | category | flops | bytes accessed | tf_op | source)
XLA Modules:
  0.0 317.9 jit_solution(9283185566868830685)
XLA Ops:
  0.0 2.5 collective-permute-start.2
  3.5 4.2 %collective-permute-start.1 = (f32[1,1,128,128]{3,2,1,0:T(8,128)S(1)}, f32[1,1,128,128]{3,2,1,0:T(8,128)S(1)}, u32[]{:S(2)}, u32[]{:S(2)}) collective-permute-start(f32[1,1,128,128]{3,2,1,0:T(8,128)S(1)} %get-tuple-element.86), channel_id=1, source_target_pairs={{0,1},{2,3},{4,5},{6,7},{8,9},{10,11},{12,13},{14,15},{16,17},{18,... | collective-permute-start | bytes 196616 | tf_op jit(solution)/shard_map/ppermute | solution.py:26
  7.8 1.3 collective-permute-start
  10.4 3.7 %collective-permute-done = f32[1,1,128,128]{3,2,1,0:T(8,128)S(1)} collective-permute-done((f32[1,1,128,128]{3,2,1,0:T(8,128)S(1)}, f32[1,1,128,128]{3,2,1,0:T(8,128)S(1)}, u32[]{:S(2)}, u32[]{:S(2)}) %collective-permute-start) | collective-permute-done | bytes 65568 | tf_op jit(solution)/shard_map/ppermute | solution.py:29
  15.0 15.7 %all_to_all.108 = f32[1,4,128,128]{3,1,0,2:T(4,128)S(1)} all-to-all(f32[1,4,128,128]{3,1,0,2:T(4,128)S(1)} %copy.21), channel_id=1, replica_groups=mesh['tm'=16,'space'=2] {'tm'}, dimensions={2} | all-to-all | bytes 524288 | tf_op jit(solution)/shard_map/all_to_all | solution.py:115
  33.1 3.6 %all-to-all-start.1 = ((f32[2,16,4,8,128]{4,3,2,0,1:T(8,128)}), f32[2,16,4,8,128]{4,3,2,0,1:T(8,128)S(1)}, u32[]{:S(2)}, u32[]{:S(2)}) async-start(f32[2,16,4,8,128]{4,3,2,0,1:T(8,128)} %copy.25), calls=%async_computation.1 | async-start | bytes 1048576 | tf_op jit(solution)/shard_map/all_to_all | solution.py:116
  36.8 14.1 %all-to-all-done.1 = f32[2,16,4,8,128]{4,3,2,0,1:T(8,128)S(1)} async-done(((f32[2,16,4,8,128]{4,3,2,0,1:T(8,128)}), f32[2,16,4,8,128]{4,3,2,0,1:T(8,128)S(1)}, u32[]{:S(2)}, u32[]{:S(2)}) %all-to-all-start.1) | async-done | bytes 524320 | tf_op jit(solution)/shard_map/all_to_all | solution.py:116
  51.1 1.6 collective-permute-start.4
  52.7 1.3 collective-permute-start.3
  54.0 1.7 collective-permute-done.4
  55.7 4.1 %collective-permute-done.3 = f32[2,1,1,128,128]{4,3,2,1,0:T(8,128)S(1)} collective-permute-done((f32[2,1,1,128,128]{4,3,2,1,0:T(8,128)S(1)}, f32[2,1,1,128,128]{4,3,2,1,0:T(8,128)S(1)}, u32[]{:S(2)}, u32[]{:S(2)}) %collective-permute-start.3) | collective-permute-done | bytes 131104 | tf_op jit(solution)/shard_map/ppermute | solution.py:29
  61.1 1.5 collective-permute-start.6
  62.5 1.3 collective-permute-start.5
  65.0 4.4 %collective-permute-done.5 = f32[2,1,1,128,128]{4,3,2,1,0:T(8,128)S(1)} collective-permute-done((f32[2,1,1,128,128]{4,3,2,1,0:T(8,128)S(1)}, f32[2,1,1,128,128]{4,3,2,1,0:T(8,128)S(1)}, u32[]{:S(2)}, u32[]{:S(2)}) %collective-permute-start.5) | collective-permute-done | bytes 131104 | tf_op jit(solution)/shard_map/ppermute | solution.py:29
  70.6 1.5 collective-permute-start.8
  72.1 1.3 collective-permute-start.7
  74.6 4.4 %collective-permute-done.7 = f32[2,1,1,128,128]{4,3,2,1,0:T(8,128)S(1)} collective-permute-done((f32[2,1,1,128,128]{4,3,2,1,0:T(8,128)S(1)}, f32[2,1,1,128,128]{4,3,2,1,0:T(8,128)S(1)}, u32[]{:S(2)}, u32[]{:S(2)}) %collective-permute-start.7) | collective-permute-done | bytes 131104 | tf_op jit(solution)/shard_map/ppermute | solution.py:29
  80.3 1.5 collective-permute-start.10
  81.8 1.3 collective-permute-start.9
  84.2 4.4 %collective-permute-done.9 = f32[2,1,1,128,128]{4,3,2,1,0:T(8,128)S(1)} collective-permute-done((f32[2,1,1,128,128]{4,3,2,1,0:T(8,128)S(1)}, f32[2,1,1,128,128]{4,3,2,1,0:T(8,128)S(1)}, u32[]{:S(2)}, u32[]{:S(2)}) %collective-permute-start.9) | collective-permute-done | bytes 131104 | tf_op jit(solution)/shard_map/ppermute | solution.py:29
  89.9 1.5 collective-permute-start.12
  91.4 1.3 collective-permute-start.11
  93.9 4.4 %collective-permute-done.11 = f32[2,1,1,128,128]{4,3,2,1,0:T(8,128)S(1)} collective-permute-done((f32[2,1,1,128,128]{4,3,2,1,0:T(8,128)S(1)}, f32[2,1,1,128,128]{4,3,2,1,0:T(8,128)S(1)}, u32[]{:S(2)}, u32[]{:S(2)}) %collective-permute-start.11) | collective-permute-done | bytes 131104 | tf_op jit(solution)/shard_map/ppermute | solution.py:29
  99.5 1.5 collective-permute-start.14
  101.0 1.3 collective-permute-start.13
  103.5 4.4 %collective-permute-done.13 = f32[2,1,1,128,128]{4,3,2,1,0:T(8,128)S(1)} collective-permute-done((f32[2,1,1,128,128]{4,3,2,1,0:T(8,128)S(1)}, f32[2,1,1,128,128]{4,3,2,1,0:T(8,128)S(1)}, u32[]{:S(2)}, u32[]{:S(2)}) %collective-permute-start.13) | collective-permute-done | bytes 131104 | tf_op jit(solution)/shard_map/ppermute | solution.py:29
  109.1 1.5 collective-permute-start.16
  110.6 1.5 collective-permute-start.15
  112.1 1.4 collective-permute-done.16
  113.5 4.7 %collective-permute-done.15 = f32[2,1,1,128,128]{4,3,2,1,0:T(8,128)S(1)} collective-permute-done((f32[2,1,1,128,128]{4,3,2,1,0:T(8,128)S(1)}, f32[2,1,1,128,128]{4,3,2,1,0:T(8,128)S(1)}, u32[]{:S(2)}, u32[]{:S(2)}) %collective-permute-start.15) | collective-permute-done | bytes 131104 | tf_op jit(solution)/shard_map/ppermute | solution.py:29
  119.4 1.5 collective-permute-start.18
  120.9 1.3 collective-permute-start.17
  123.4 4.4 %collective-permute-done.17 = f32[2,1,1,128,128]{4,3,2,1,0:T(8,128)S(1)} collective-permute-done((f32[2,1,1,128,128]{4,3,2,1,0:T(8,128)S(1)}, f32[2,1,1,128,128]{4,3,2,1,0:T(8,128)S(1)}, u32[]{:S(2)}, u32[]{:S(2)}) %collective-permute-start.17) | collective-permute-done | bytes 131104 | tf_op jit(solution)/shard_map/ppermute | solution.py:29
  129.4 18.5 %all_to_all.109 = f32[2,1,4,128,128]{4,2,1,0,3:T(4,128)S(1)} all-to-all(f32[2,1,4,128,128]{4,2,1,0,3:T(4,128)S(1)} %copy.27), channel_id=1, replica_groups=mesh['tm'=16,'space'=2] {'tm'}, dimensions={3} | all-to-all | bytes 1048576 | tf_op jit(solution)/shard_map/all_to_all | solution.py:126
  149.1 14.0 %all_to_all.110 = f32[16,4,8,128]{3,2,1,0:T(8,128)S(1)} all-to-all(f32[16,4,8,128]{3,2,1,0:T(8,128)S(1)} %bitcast.743), channel_id=1, replica_groups=mesh['tm'=16,'space'=2] {'tm'}, dimensions={0} | all-to-all | bytes 524288 | tf_op jit(solution)/shard_map/all_to_all | solution.py:132
  163.1 1.8 collective-permute-start.21
  164.9 1.5 collective-permute-start.20
  166.4 1.3 collective-permute-start.19
  168.3 4.3 %collective-permute-done.19 = f32[1,1,128,128]{3,2,1,0:T(8,128)S(1)} collective-permute-done((f32[1,1,128,128]{3,2,1,0:T(8,128)S(1)}, f32[1,1,128,128]{3,2,1,0:T(8,128)S(1)}, u32[]{:S(2)}, u32[]{:S(2)}) %collective-permute-start.19) | collective-permute-done | bytes 65568 | tf_op jit(solution)/shard_map/ppermute | solution.py:29
  173.4 13.0 %all_to_all.111 = f32[1,4,128,128]{3,1,0,2:T(4,128)S(1)} all-to-all(f32[1,4,128,128]{3,1,0,2:T(4,128)S(1)} %copy.30), channel_id=1, replica_groups=mesh['tm'=16,'space'=2] {'tm'}, dimensions={2} | all-to-all | bytes 524288 | tf_op jit(solution)/shard_map/all_to_all | solution.py:115
  188.0 17.0 %all_to_all.112 = f32[2,16,4,8,128]{4,3,2,0,1:T(8,128)S(1)} all-to-all(f32[2,16,4,8,128]{4,3,2,0,1:T(8,128)S(1)} %copy.34), channel_id=1, replica_groups=mesh['tm'=16,'space'=2] {'tm'}, dimensions={1} | all-to-all | bytes 1048576 | tf_op jit(solution)/shard_map/all_to_all | solution.py:116
  205.2 1.6 collective-permute-start.23
  208.1 1.7 collective-permute-done.23
  209.8 4.1 %collective-permute-done.22 = f32[2,1,1,128,128]{4,3,2,1,0:T(8,128)S(1)} collective-permute-done((f32[2,1,1,128,128]{4,3,2,1,0:T(8,128)S(1)}, f32[2,1,1,128,128]{4,3,2,1,0:T(8,128)S(1)}, u32[]{:S(2)}, u32[]{:S(2)}) %collective-permute-start.22) | collective-permute-done | bytes 131104 | tf_op jit(solution)/shard_map/ppermute | solution.py:29
  215.2 1.5 collective-permute-start.25
  219.1 4.4 %collective-permute-done.24 = f32[2,1,1,128,128]{4,3,2,1,0:T(8,128)S(1)} collective-permute-done((f32[2,1,1,128,128]{4,3,2,1,0:T(8,128)S(1)}, f32[2,1,1,128,128]{4,3,2,1,0:T(8,128)S(1)}, u32[]{:S(2)}, u32[]{:S(2)}) %collective-permute-start.24) | collective-permute-done | bytes 131104 | tf_op jit(solution)/shard_map/ppermute | solution.py:29
  224.8 1.5 collective-permute-start.27
  228.7 4.4 %collective-permute-done.26 = f32[2,1,1,128,128]{4,3,2,1,0:T(8,128)S(1)} collective-permute-done((f32[2,1,1,128,128]{4,3,2,1,0:T(8,128)S(1)}, f32[2,1,1,128,128]{4,3,2,1,0:T(8,128)S(1)}, u32[]{:S(2)}, u32[]{:S(2)}) %collective-permute-start.26) | collective-permute-done | bytes 131104 | tf_op jit(solution)/shard_map/ppermute | solution.py:29
  234.4 1.5 collective-permute-start.29
  235.9 1.5 collective-permute-start.28
  238.4 4.4 %collective-permute-done.28 = f32[2,1,1,128,128]{4,3,2,1,0:T(8,128)S(1)} collective-permute-done((f32[2,1,1,128,128]{4,3,2,1,0:T(8,128)S(1)}, f32[2,1,1,128,128]{4,3,2,1,0:T(8,128)S(1)}, u32[]{:S(2)}, u32[]{:S(2)}) %collective-permute-start.28) | collective-permute-done | bytes 131104 | tf_op jit(solution)/shard_map/ppermute | solution.py:29
  244.0 1.5 collective-permute-start.31
  248.0 4.4 %collective-permute-done.30 = f32[2,1,1,128,128]{4,3,2,1,0:T(8,128)S(1)} collective-permute-done((f32[2,1,1,128,128]{4,3,2,1,0:T(8,128)S(1)}, f32[2,1,1,128,128]{4,3,2,1,0:T(8,128)S(1)}, u32[]{:S(2)}, u32[]{:S(2)}) %collective-permute-start.30) | collective-permute-done | bytes 131104 | tf_op jit(solution)/shard_map/ppermute | solution.py:29
  253.6 1.5 collective-permute-start.33
  255.1 1.3 collective-permute-start.32
  257.6 4.4 %collective-permute-done.32 = f32[2,1,1,128,128]{4,3,2,1,0:T(8,128)S(1)} collective-permute-done((f32[2,1,1,128,128]{4,3,2,1,0:T(8,128)S(1)}, f32[2,1,1,128,128]{4,3,2,1,0:T(8,128)S(1)}, u32[]{:S(2)}, u32[]{:S(2)}) %collective-permute-start.32) | collective-permute-done | bytes 131104 | tf_op jit(solution)/shard_map/ppermute | solution.py:29
  263.2 1.5 collective-permute-start.35
  264.7 1.3 collective-permute-start.34
  266.0 1.6 collective-permute-done.35
  267.6 4.7 %collective-permute-done.34 = f32[2,1,1,128,128]{4,3,2,1,0:T(8,128)S(1)} collective-permute-done((f32[2,1,1,128,128]{4,3,2,1,0:T(8,128)S(1)}, f32[2,1,1,128,128]{4,3,2,1,0:T(8,128)S(1)}, u32[]{:S(2)}, u32[]{:S(2)}) %collective-permute-start.34) | collective-permute-done | bytes 131104 | tf_op jit(solution)/shard_map/ppermute | solution.py:29
  273.5 1.5 collective-permute-start.37
  277.5 4.4 %collective-permute-done.36 = f32[2,1,1,128,128]{4,3,2,1,0:T(8,128)S(1)} collective-permute-done((f32[2,1,1,128,128]{4,3,2,1,0:T(8,128)S(1)}, f32[2,1,1,128,128]{4,3,2,1,0:T(8,128)S(1)}, u32[]{:S(2)}, u32[]{:S(2)}) %collective-permute-start.36) | collective-permute-done | bytes 131104 | tf_op jit(solution)/shard_map/ppermute | solution.py:29
  283.5 18.5 %all_to_all.113 = f32[2,1,4,128,128]{4,2,1,0,3:T(4,128)S(1)} all-to-all(f32[2,1,4,128,128]{4,2,1,0,3:T(4,128)S(1)} %copy.36), channel_id=1, replica_groups=mesh['tm'=16,'space'=2] {'tm'}, dimensions={3} | all-to-all | bytes 1048576 | tf_op jit(solution)/shard_map/all_to_all | solution.py:126
  303.2 14.0 %all_to_all.114 = f32[16,4,8,128]{3,2,1,0:T(8,128)S(1)} all-to-all(f32[16,4,8,128]{3,2,1,0:T(8,128)S(1)} %bitcast.748), channel_id=1, replica_groups=mesh['tm'=16,'space'=2] {'tm'}, dimensions={0} | all-to-all | bytes 524288 | tf_op jit(solution)/shard_map/all_to_all | solution.py:132
  (142 shorter events, 52.8 us)
Async XLA Ops:
  0.0 14.1 %copy-start.1 = (f32[4,128,128]{2,1,0:T(8,128)S(1)}, f32[4,128,128]{2,1,0:T(8,128)}, u32[]{:S(2)}) copy-start(f32[4,128,128]{2,1,0:T(8,128)} %param.5) | copy-start | bytes 786436
  0.0 14.4 %collective-permute-start.2 = (f32[4,128,128]{2,1,0:T(8,128)}, f32[4,128,128]{2,1,0:T(8,128)S(1)}, u32[]{:S(2)}, u32[]{:S(2)}) collective-permute-start(f32[4,128,128]{2,1,0:T(8,128)} %param.5), channel_id=1, source_target_pairs={{0,2},{2,4},{4,6},{6,8},{8,10},{10,12},{12,14},{14,16},{16,18},{18... | collective-permute-start | bytes 786440 | tf_op jit(solution)/shard_map/ppermute | solution.py:18
  2.5 11.9 %copy-start = (f32[4,128,128]{2,1,0:T(8,128)S(1)}, f32[4,128,128]{2,1,0:T(8,128)}, u32[]{:S(2)}) copy-start(f32[4,128,128]{2,1,0:T(8,128)} %param.6) | copy-start | bytes 786436
  2.6 11.9 %copy-start.2 = (f32[1,4,128,128]{3,2,1,0:T(8,128)S(1)}, f32[1,4,128,128]{3,2,1,0:T(8,128)}, u32[]{:S(2)}) copy-start(f32[1,4,128,128]{3,2,1,0:T(8,128)} %param.4) | copy-start | bytes 786436
  3.5 6.9 %collective-permute-start.1 = (f32[1,1,128,128]{3,2,1,0:T(8,128)S(1)}, f32[1,1,128,128]{3,2,1,0:T(8,128)S(1)}, u32[]{:S(2)}, u32[]{:S(2)}) collective-permute-start(f32[1,1,128,128]{3,2,1,0:T(8,128)S(1)} %get-tuple-element.86), channel_id=1, source_target_pairs={{0,1},{2,3},{4,5},{6,7},{8,9},{10,11},{12,13},{14,15},{16,17},{18,... | collective-permute-start | bytes 196616 | tf_op jit(solution)/shard_map/ppermute | solution.py:26
  7.8 6.4 %collective-permute-start = (f32[1,1,128,128]{3,2,1,0:T(8,128)S(1)}, f32[1,1,128,128]{3,2,1,0:T(8,128)S(1)}, u32[]{:S(2)}, u32[]{:S(2)}) collective-permute-start(f32[1,1,128,128]{3,2,1,0:T(8,128)S(1)} %get-tuple-element.87), channel_id=1, source_target_pairs={{1,0},{3,2},{5,4},{7,6},{9,8},{11,10},{13,12},{15,14},{17,16},{19,... | collective-permute-start | bytes 196616 | tf_op jit(solution)/shard_map/ppermute | solution.py:29
  33.1 17.8 %all-to-all-start.1 = ((f32[2,16,4,8,128]{4,3,2,0,1:T(8,128)}), f32[2,16,4,8,128]{4,3,2,0,1:T(8,128)S(1)}, u32[]{:S(2)}, u32[]{:S(2)}) async-start(f32[2,16,4,8,128]{4,3,2,0,1:T(8,128)} %copy.25), calls=%async_computation.1 | async-start | bytes 1048576 | tf_op jit(solution)/shard_map/all_to_all | solution.py:116
  51.1 4.6 %collective-permute-start.4 = (f32[2,1,1,128,128]{4,3,2,1,0:T(8,128)S(1)}, f32[2,1,1,128,128]{4,3,2,1,0:T(8,128)S(1)}, u32[]{:S(2)}, u32[]{:S(2)}) collective-permute-start(f32[2,1,1,128,128]{4,3,2,1,0:T(8,128)S(1)} %get-tuple-element.82), channel_id=1, source_target_pairs={{0,1},{2,3},{4,5},{6,7},{8,9},{10,11},{12,13},{14,15},{16,17},{18,... | collective-permute-start | bytes 393224 | tf_op jit(solution)/shard_map/ppermute | solution.py:26
  52.7 7.1 %collective-permute-start.3 = (f32[2,1,1,128,128]{4,3,2,1,0:T(8,128)S(1)}, f32[2,1,1,128,128]{4,3,2,1,0:T(8,128)S(1)}, u32[]{:S(2)}, u32[]{:S(2)}) collective-permute-start(f32[2,1,1,128,128]{4,3,2,1,0:T(8,128)S(1)} %get-tuple-element.83), channel_id=1, source_target_pairs={{1,0},{3,2},{5,4},{7,6},{9,8},{11,10},{13,12},{15,14},{17,16},{19,... | collective-permute-start | bytes 393224 | tf_op jit(solution)/shard_map/ppermute | solution.py:29
  61.1 4.0 %collective-permute-start.6 = (f32[2,1,1,128,128]{4,3,2,1,0:T(8,128)S(1)}, f32[2,1,1,128,128]{4,3,2,1,0:T(8,128)S(1)}, u32[]{:S(2)}, u32[]{:S(2)}) collective-permute-start(f32[2,1,1,128,128]{4,3,2,1,0:T(8,128)S(1)} %get-tuple-element.80), channel_id=1, source_target_pairs={{0,1},{2,3},{4,5},{6,7},{8,9},{10,11},{12,13},{14,15},{16,17},{18,... | collective-permute-start | bytes 393224 | tf_op jit(solution)/shard_map/ppermute | solution.py:26
  62.5 6.9 %collective-permute-start.5 = (f32[2,1,1,128,128]{4,3,2,1,0:T(8,128)S(1)}, f32[2,1,1,128,128]{4,3,2,1,0:T(8,128)S(1)}, u32[]{:S(2)}, u32[]{:S(2)}) collective-permute-start(f32[2,1,1,128,128]{4,3,2,1,0:T(8,128)S(1)} %get-tuple-element.81), channel_id=1, source_target_pairs={{1,0},{3,2},{5,4},{7,6},{9,8},{11,10},{13,12},{15,14},{17,16},{19,... | collective-permute-start | bytes 393224 | tf_op jit(solution)/shard_map/ppermute | solution.py:29
  70.6 4.0 %collective-permute-start.8 = (f32[2,1,1,128,128]{4,3,2,1,0:T(8,128)S(1)}, f32[2,1,1,128,128]{4,3,2,1,0:T(8,128)S(1)}, u32[]{:S(2)}, u32[]{:S(2)}) collective-permute-start(f32[2,1,1,128,128]{4,3,2,1,0:T(8,128)S(1)} %get-tuple-element.78), channel_id=1, source_target_pairs={{0,1},{2,3},{4,5},{6,7},{8,9},{10,11},{12,13},{14,15},{16,17},{18,... | collective-permute-start | bytes 393224 | tf_op jit(solution)/shard_map/ppermute | solution.py:26
  72.1 6.9 %collective-permute-start.7 = (f32[2,1,1,128,128]{4,3,2,1,0:T(8,128)S(1)}, f32[2,1,1,128,128]{4,3,2,1,0:T(8,128)S(1)}, u32[]{:S(2)}, u32[]{:S(2)}) collective-permute-start(f32[2,1,1,128,128]{4,3,2,1,0:T(8,128)S(1)} %get-tuple-element.79), channel_id=1, source_target_pairs={{1,0},{3,2},{5,4},{7,6},{9,8},{11,10},{13,12},{15,14},{17,16},{19,... | collective-permute-start | bytes 393224 | tf_op jit(solution)/shard_map/ppermute | solution.py:29
  80.3 4.0 %collective-permute-start.10 = (f32[2,1,1,128,128]{4,3,2,1,0:T(8,128)S(1)}, f32[2,1,1,128,128]{4,3,2,1,0:T(8,128)S(1)}, u32[]{:S(2)}, u32[]{:S(2)}) collective-permute-start(f32[2,1,1,128,128]{4,3,2,1,0:T(8,128)S(1)} %get-tuple-element.76), channel_id=1, source_target_pairs={{0,1},{2,3},{4,5},{6,7},{8,9},{10,11},{12,13},{14,15},{16,17},{18,... | collective-permute-start | bytes 393224 | tf_op jit(solution)/shard_map/ppermute | solution.py:26
  81.8 6.9 %collective-permute-start.9 = (f32[2,1,1,128,128]{4,3,2,1,0:T(8,128)S(1)}, f32[2,1,1,128,128]{4,3,2,1,0:T(8,128)S(1)}, u32[]{:S(2)}, u32[]{:S(2)}) collective-permute-start(f32[2,1,1,128,128]{4,3,2,1,0:T(8,128)S(1)} %get-tuple-element.77), channel_id=1, source_target_pairs={{1,0},{3,2},{5,4},{7,6},{9,8},{11,10},{13,12},{15,14},{17,16},{19,... | collective-permute-start | bytes 393224 | tf_op jit(solution)/shard_map/ppermute | solution.py:29
  89.9 4.0 %collective-permute-start.12 = (f32[2,1,1,128,128]{4,3,2,1,0:T(8,128)S(1)}, f32[2,1,1,128,128]{4,3,2,1,0:T(8,128)S(1)}, u32[]{:S(2)}, u32[]{:S(2)}) collective-permute-start(f32[2,1,1,128,128]{4,3,2,1,0:T(8,128)S(1)} %get-tuple-element.74), channel_id=1, source_target_pairs={{0,1},{2,3},{4,5},{6,7},{8,9},{10,11},{12,13},{14,15},{16,17},{18,... | collective-permute-start | bytes 393224 | tf_op jit(solution)/shard_map/ppermute | solution.py:26
  91.4 6.9 %collective-permute-start.11 = (f32[2,1,1,128,128]{4,3,2,1,0:T(8,128)S(1)}, f32[2,1,1,128,128]{4,3,2,1,0:T(8,128)S(1)}, u32[]{:S(2)}, u32[]{:S(2)}) collective-permute-start(f32[2,1,1,128,128]{4,3,2,1,0:T(8,128)S(1)} %get-tuple-element.75), channel_id=1, source_target_pairs={{1,0},{3,2},{5,4},{7,6},{9,8},{11,10},{13,12},{15,14},{17,16},{19,... | collective-permute-start | bytes 393224 | tf_op jit(solution)/shard_map/ppermute | solution.py:29
  99.5 4.0 %collective-permute-start.14 = (f32[2,1,1,128,128]{4,3,2,1,0:T(8,128)S(1)}, f32[2,1,1,128,128]{4,3,2,1,0:T(8,128)S(1)}, u32[]{:S(2)}, u32[]{:S(2)}) collective-permute-start(f32[2,1,1,128,128]{4,3,2,1,0:T(8,128)S(1)} %get-tuple-element.72), channel_id=1, source_target_pairs={{0,1},{2,3},{4,5},{6,7},{8,9},{10,11},{12,13},{14,15},{16,17},{18,... | collective-permute-start | bytes 393224 | tf_op jit(solution)/shard_map/ppermute | solution.py:26
  101.0 6.9 %collective-permute-start.13 = (f32[2,1,1,128,128]{4,3,2,1,0:T(8,128)S(1)}, f32[2,1,1,128,128]{4,3,2,1,0:T(8,128)S(1)}, u32[]{:S(2)}, u32[]{:S(2)}) collective-permute-start(f32[2,1,1,128,128]{4,3,2,1,0:T(8,128)S(1)} %get-tuple-element.73), channel_id=1, source_target_pairs={{1,0},{3,2},{5,4},{7,6},{9,8},{11,10},{13,12},{15,14},{17,16},{19,... | collective-permute-start | bytes 393224 | tf_op jit(solution)/shard_map/ppermute | solution.py:29
  109.1 4.4 %collective-permute-start.16 = (f32[2,1,1,128,128]{4,3,2,1,0:T(8,128)S(1)}, f32[2,1,1,128,128]{4,3,2,1,0:T(8,128)S(1)}, u32[]{:S(2)}, u32[]{:S(2)}) collective-permute-start(f32[2,1,1,128,128]{4,3,2,1,0:T(8,128)S(1)} %get-tuple-element.70), channel_id=1, source_target_pairs={{0,1},{2,3},{4,5},{6,7},{8,9},{10,11},{12,13},{14,15},{16,17},{18,... | collective-permute-start | bytes 393224 | tf_op jit(solution)/shard_map/ppermute | solution.py:26
  110.6 7.6 %collective-permute-start.15 = (f32[2,1,1,128,128]{4,3,2,1,0:T(8,128)S(1)}, f32[2,1,1,128,128]{4,3,2,1,0:T(8,128)S(1)}, u32[]{:S(2)}, u32[]{:S(2)}) collective-permute-start(f32[2,1,1,128,128]{4,3,2,1,0:T(8,128)S(1)} %get-tuple-element.71), channel_id=1, source_target_pairs={{1,0},{3,2},{5,4},{7,6},{9,8},{11,10},{13,12},{15,14},{17,16},{19,... | collective-permute-start | bytes 393224 | tf_op jit(solution)/shard_map/ppermute | solution.py:29
  119.4 4.0 %collective-permute-start.18 = (f32[2,1,1,128,128]{4,3,2,1,0:T(8,128)S(1)}, f32[2,1,1,128,128]{4,3,2,1,0:T(8,128)S(1)}, u32[]{:S(2)}, u32[]{:S(2)}) collective-permute-start(f32[2,1,1,128,128]{4,3,2,1,0:T(8,128)S(1)} %get-tuple-element.68), channel_id=1, source_target_pairs={{0,1},{2,3},{4,5},{6,7},{8,9},{10,11},{12,13},{14,15},{16,17},{18,... | collective-permute-start | bytes 393224 | tf_op jit(solution)/shard_map/ppermute | solution.py:26
  120.9 6.9 %collective-permute-start.17 = (f32[2,1,1,128,128]{4,3,2,1,0:T(8,128)S(1)}, f32[2,1,1,128,128]{4,3,2,1,0:T(8,128)S(1)}, u32[]{:S(2)}, u32[]{:S(2)}) collective-permute-start(f32[2,1,1,128,128]{4,3,2,1,0:T(8,128)S(1)} %get-tuple-element.69), channel_id=1, source_target_pairs={{1,0},{3,2},{5,4},{7,6},{9,8},{11,10},{13,12},{15,14},{17,16},{19,... | collective-permute-start | bytes 393224 | tf_op jit(solution)/shard_map/ppermute | solution.py:29
  163.1 9.8 %collective-permute-start.21 = (f32[4,128,128]{2,1,0:T(8,128)S(1)}, f32[4,128,128]{2,1,0:T(8,128)S(1)}, u32[]{:S(2)}, u32[]{:S(2)}) collective-permute-start(f32[4,128,128]{2,1,0:T(8,128)S(1)} %bitcast_add_fusion.1), channel_id=1, source_target_pairs={{0,2},{2,4},{4,6},{6,8},{8,10},{10,12},{12,14},{14,16},{16,18},{18... | collective-permute-start | bytes 786440 | tf_op jit(solution)/shard_map/ppermute | solution.py:18
  164.9 3.4 %collective-permute-start.20 = (f32[1,1,128,128]{3,2,1,0:T(8,128)S(1)}, f32[1,1,128,128]{3,2,1,0:T(8,128)S(1)}, u32[]{:S(2)}, u32[]{:S(2)}) collective-permute-start(f32[1,1,128,128]{3,2,1,0:T(8,128)S(1)} %get-tuple-element.84), channel_id=1, source_target_pairs={{0,1},{2,3},{4,5},{6,7},{8,9},{10,11},{12,13},{14,15},{16,17},{18,... | collective-permute-start | bytes 196616 | tf_op jit(solution)/shard_map/ppermute | solution.py:26
  166.4 6.2 %collective-permute-start.19 = (f32[1,1,128,128]{3,2,1,0:T(8,128)S(1)}, f32[1,1,128,128]{3,2,1,0:T(8,128)S(1)}, u32[]{:S(2)}, u32[]{:S(2)}) collective-permute-start(f32[1,1,128,128]{3,2,1,0:T(8,128)S(1)} %get-tuple-element.85), channel_id=1, source_target_pairs={{1,0},{3,2},{5,4},{7,6},{9,8},{11,10},{13,12},{15,14},{17,16},{19,... | collective-permute-start | bytes 196616 | tf_op jit(solution)/shard_map/ppermute | solution.py:29
  205.2 4.6 %collective-permute-start.23 = (f32[2,1,1,128,128]{4,3,2,1,0:T(8,128)S(1)}, f32[2,1,1,128,128]{4,3,2,1,0:T(8,128)S(1)}, u32[]{:S(2)}, u32[]{:S(2)}) collective-permute-start(f32[2,1,1,128,128]{4,3,2,1,0:T(8,128)S(1)} %get-tuple-element.64), channel_id=1, source_target_pairs={{0,1},{2,3},{4,5},{6,7},{8,9},{10,11},{12,13},{14,15},{16,17},{18,... | collective-permute-start | bytes 393224 | tf_op jit(solution)/shard_map/ppermute | solution.py:26
  206.8 7.2 %collective-permute-start.22 = (f32[2,1,1,128,128]{4,3,2,1,0:T(8,128)S(1)}, f32[2,1,1,128,128]{4,3,2,1,0:T(8,128)S(1)}, u32[]{:S(2)}, u32[]{:S(2)}) collective-permute-start(f32[2,1,1,128,128]{4,3,2,1,0:T(8,128)S(1)} %get-tuple-element.65), channel_id=1, source_target_pairs={{1,0},{3,2},{5,4},{7,6},{9,8},{11,10},{13,12},{15,14},{17,16},{19,... | collective-permute-start | bytes 393224 | tf_op jit(solution)/shard_map/ppermute | solution.py:29
  215.2 4.0 %collective-permute-start.25 = (f32[2,1,1,128,128]{4,3,2,1,0:T(8,128)S(1)}, f32[2,1,1,128,128]{4,3,2,1,0:T(8,128)S(1)}, u32[]{:S(2)}, u32[]{:S(2)}) collective-permute-start(f32[2,1,1,128,128]{4,3,2,1,0:T(8,128)S(1)} %get-tuple-element.62), channel_id=1, source_target_pairs={{0,1},{2,3},{4,5},{6,7},{8,9},{10,11},{12,13},{14,15},{16,17},{18,... | collective-permute-start | bytes 393224 | tf_op jit(solution)/shard_map/ppermute | solution.py:26
  216.6 6.9 %collective-permute-start.24 = (f32[2,1,1,128,128]{4,3,2,1,0:T(8,128)S(1)}, f32[2,1,1,128,128]{4,3,2,1,0:T(8,128)S(1)}, u32[]{:S(2)}, u32[]{:S(2)}) collective-permute-start(f32[2,1,1,128,128]{4,3,2,1,0:T(8,128)S(1)} %get-tuple-element.63), channel_id=1, source_target_pairs={{1,0},{3,2},{5,4},{7,6},{9,8},{11,10},{13,12},{15,14},{17,16},{19,... | collective-permute-start | bytes 393224 | tf_op jit(solution)/shard_map/ppermute | solution.py:29
  224.8 4.0 %collective-permute-start.27 = (f32[2,1,1,128,128]{4,3,2,1,0:T(8,128)S(1)}, f32[2,1,1,128,128]{4,3,2,1,0:T(8,128)S(1)}, u32[]{:S(2)}, u32[]{:S(2)}) collective-permute-start(f32[2,1,1,128,128]{4,3,2,1,0:T(8,128)S(1)} %get-tuple-element.60), channel_id=1, source_target_pairs={{0,1},{2,3},{4,5},{6,7},{8,9},{10,11},{12,13},{14,15},{16,17},{18,... | collective-permute-start | bytes 393224 | tf_op jit(solution)/shard_map/ppermute | solution.py:26
  226.3 6.9 %collective-permute-start.26 = (f32[2,1,1,128,128]{4,3,2,1,0:T(8,128)S(1)}, f32[2,1,1,128,128]{4,3,2,1,0:T(8,128)S(1)}, u32[]{:S(2)}, u32[]{:S(2)}) collective-permute-start(f32[2,1,1,128,128]{4,3,2,1,0:T(8,128)S(1)} %get-tuple-element.61), channel_id=1, source_target_pairs={{1,0},{3,2},{5,4},{7,6},{9,8},{11,10},{13,12},{15,14},{17,16},{19,... | collective-permute-start | bytes 393224 | tf_op jit(solution)/shard_map/ppermute | solution.py:29
  234.4 4.0 %collective-permute-start.29 = (f32[2,1,1,128,128]{4,3,2,1,0:T(8,128)S(1)}, f32[2,1,1,128,128]{4,3,2,1,0:T(8,128)S(1)}, u32[]{:S(2)}, u32[]{:S(2)}) collective-permute-start(f32[2,1,1,128,128]{4,3,2,1,0:T(8,128)S(1)} %get-tuple-element.58), channel_id=1, source_target_pairs={{0,1},{2,3},{4,5},{6,7},{8,9},{10,11},{12,13},{14,15},{16,17},{18,... | collective-permute-start | bytes 393224 | tf_op jit(solution)/shard_map/ppermute | solution.py:26
  235.9 6.9 %collective-permute-start.28 = (f32[2,1,1,128,128]{4,3,2,1,0:T(8,128)S(1)}, f32[2,1,1,128,128]{4,3,2,1,0:T(8,128)S(1)}, u32[]{:S(2)}, u32[]{:S(2)}) collective-permute-start(f32[2,1,1,128,128]{4,3,2,1,0:T(8,128)S(1)} %get-tuple-element.59), channel_id=1, source_target_pairs={{1,0},{3,2},{5,4},{7,6},{9,8},{11,10},{13,12},{15,14},{17,16},{19,... | collective-permute-start | bytes 393224 | tf_op jit(solution)/shard_map/ppermute | solution.py:29
  244.0 4.0 %collective-permute-start.31 = (f32[2,1,1,128,128]{4,3,2,1,0:T(8,128)S(1)}, f32[2,1,1,128,128]{4,3,2,1,0:T(8,128)S(1)}, u32[]{:S(2)}, u32[]{:S(2)}) collective-permute-start(f32[2,1,1,128,128]{4,3,2,1,0:T(8,128)S(1)} %get-tuple-element.56), channel_id=1, source_target_pairs={{0,1},{2,3},{4,5},{6,7},{8,9},{10,11},{12,13},{14,15},{16,17},{18,... | collective-permute-start | bytes 393224 | tf_op jit(solution)/shard_map/ppermute | solution.py:26
  245.5 6.9 %collective-permute-start.30 = (f32[2,1,1,128,128]{4,3,2,1,0:T(8,128)S(1)}, f32[2,1,1,128,128]{4,3,2,1,0:T(8,128)S(1)}, u32[]{:S(2)}, u32[]{:S(2)}) collective-permute-start(f32[2,1,1,128,128]{4,3,2,1,0:T(8,128)S(1)} %get-tuple-element.57), channel_id=1, source_target_pairs={{1,0},{3,2},{5,4},{7,6},{9,8},{11,10},{13,12},{15,14},{17,16},{19,... | collective-permute-start | bytes 393224 | tf_op jit(solution)/shard_map/ppermute | solution.py:29
  253.6 4.0 %collective-permute-start.33 = (f32[2,1,1,128,128]{4,3,2,1,0:T(8,128)S(1)}, f32[2,1,1,128,128]{4,3,2,1,0:T(8,128)S(1)}, u32[]{:S(2)}, u32[]{:S(2)}) collective-permute-start(f32[2,1,1,128,128]{4,3,2,1,0:T(8,128)S(1)} %get-tuple-element.54), channel_id=1, source_target_pairs={{0,1},{2,3},{4,5},{6,7},{8,9},{10,11},{12,13},{14,15},{16,17},{18,... | collective-permute-start | bytes 393224 | tf_op jit(solution)/shard_map/ppermute | solution.py:26
  255.1 6.9 %collective-permute-start.32 = (f32[2,1,1,128,128]{4,3,2,1,0:T(8,128)S(1)}, f32[2,1,1,128,128]{4,3,2,1,0:T(8,128)S(1)}, u32[]{:S(2)}, u32[]{:S(2)}) collective-permute-start(f32[2,1,1,128,128]{4,3,2,1,0:T(8,128)S(1)} %get-tuple-element.55), channel_id=1, source_target_pairs={{1,0},{3,2},{5,4},{7,6},{9,8},{11,10},{13,12},{15,14},{17,16},{19,... | collective-permute-start | bytes 393224 | tf_op jit(solution)/shard_map/ppermute | solution.py:29
  263.2 4.4 %collective-permute-start.35 = (f32[2,1,1,128,128]{4,3,2,1,0:T(8,128)S(1)}, f32[2,1,1,128,128]{4,3,2,1,0:T(8,128)S(1)}, u32[]{:S(2)}, u32[]{:S(2)}) collective-permute-start(f32[2,1,1,128,128]{4,3,2,1,0:T(8,128)S(1)} %get-tuple-element.52), channel_id=1, source_target_pairs={{0,1},{2,3},{4,5},{6,7},{8,9},{10,11},{12,13},{14,15},{16,17},{18,... | collective-permute-start | bytes 393224 | tf_op jit(solution)/shard_map/ppermute | solution.py:26
  264.7 7.6 %collective-permute-start.34 = (f32[2,1,1,128,128]{4,3,2,1,0:T(8,128)S(1)}, f32[2,1,1,128,128]{4,3,2,1,0:T(8,128)S(1)}, u32[]{:S(2)}, u32[]{:S(2)}) collective-permute-start(f32[2,1,1,128,128]{4,3,2,1,0:T(8,128)S(1)} %get-tuple-element.53), channel_id=1, source_target_pairs={{1,0},{3,2},{5,4},{7,6},{9,8},{11,10},{13,12},{15,14},{17,16},{19,... | collective-permute-start | bytes 393224 | tf_op jit(solution)/shard_map/ppermute | solution.py:29
  273.5 4.0 %collective-permute-start.37 = (f32[2,1,1,128,128]{4,3,2,1,0:T(8,128)S(1)}, f32[2,1,1,128,128]{4,3,2,1,0:T(8,128)S(1)}, u32[]{:S(2)}, u32[]{:S(2)}) collective-permute-start(f32[2,1,1,128,128]{4,3,2,1,0:T(8,128)S(1)} %get-tuple-element.50), channel_id=1, source_target_pairs={{0,1},{2,3},{4,5},{6,7},{8,9},{10,11},{12,13},{14,15},{16,17},{18,... | collective-permute-start | bytes 393224 | tf_op jit(solution)/shard_map/ppermute | solution.py:26
  275.0 6.9 %collective-permute-start.36 = (f32[2,1,1,128,128]{4,3,2,1,0:T(8,128)S(1)}, f32[2,1,1,128,128]{4,3,2,1,0:T(8,128)S(1)}, u32[]{:S(2)}, u32[]{:S(2)}) collective-permute-start(f32[2,1,1,128,128]{4,3,2,1,0:T(8,128)S(1)} %get-tuple-element.51), channel_id=1, source_target_pairs={{1,0},{3,2},{5,4},{7,6},{9,8},{11,10},{13,12},{15,14},{17,16},{19,... | collective-permute-start | bytes 393224 | tf_op jit(solution)/shard_map/ppermute | solution.py:29
where the time goes:
time: 319 us; the launch traced here: 318 us
  waiting for transfers between devices  113 us (35%)
  blocking collectives  111 us (35%)
  starting transfers between devices  61.2 us (19%)
  other arithmetic  23.6 us (7%)
  local copies, waits for them, and re-layouts  4.47 us (1%)
  matrix products  3.5 us (1%)
    ppermute x18, waiting for transfers between devices, with_halo(): lax.ppermute(lax.slice_in_dim(block, 0, width, axis=dim), axis, backward)  78 us
    all_to_all x2, blocking collectives, body(): lax.all_to_all(solved, 'tm', split_axis=3, concat_axis=1, tiled=True)  37 us
    ppermute x18, starting transfers between devices, with_halo(): lax.ppermute(lax.slice_in_dim(block, block.shape[dim] - width, None, axis...  29.6 us
    all_to_all x2, blocking collectives, body(): lax.all_to_all(scaled, 'tm', split_axis=2, concat_axis=0, tiled=True)  28.7 us
    all_to_all x2, blocking collectives, body(): lax.all_to_all(inverse_part, 'tm', split_axis=0, concat_axis=2, tiled=True)  28 us
    ppermute x18, starting transfers between devices, with_halo(): lax.ppermute(lax.slice_in_dim(block, 0, width, axis=dim), axis, backward)  23.7 us
    ppermute x18, waiting for transfers between devices, with_halo(): lax.ppermute(lax.slice_in_dim(block, block.shape[dim] - width, None, axis...  21.2 us
    all_to_all x1, blocking collectives, body(): lax.all_to_all(spectrum, 'tm', split_axis=1, concat_axis=3, tiled=True)  17 us
  transfers between devices with their start and end apart: 39, of which 36 were waited for; matrix products, arithmetic and copies ran while one was open for 1% of the time, Pallas kernels for 0%

commit v1 on v0

--- a/solution.py
+++ b/solution.py
@@ -1,15 +1,392 @@
+import functools
 import math
 
 import jax
 import jax.numpy as jnp
 from jax import lax
+from jax.experimental import pallas as pl
+from jax.experimental.pallas import tpu as pltpu
 from jax.sharding import PartitionSpec as P
 
 ITERS = 2
 SWEEPS = 8
 
-
 wrap_alpha = 0.1
+
+APPS = SWEEPS + 1
+HALO = ITERS * APPS - 1
+LANES = 128
+SUB = 8
+
+
+def position(site):
+    a, b = site // 2, site % 2
+    return 2 * a + (b ^ (a % 2))
+
+
+def vmem_call(kernel, out_shapes, n_in, scratch=(), n_smem=0, flops=0, limit=None, name=None):
+    specs = [pl.BlockSpec(memory_space=pltpu.SMEM)] * n_smem
+    specs += [pl.BlockSpec(memory_space=pltpu.VMEM)] * n_in
+    multi = isinstance(out_shapes, (tuple, list))
+    outs = pl.BlockSpec(memory_space=pltpu.VMEM)
+    return pl.pallas_call(
+        kernel,
+        out_shape=out_shapes,
+        in_specs=specs,
+        out_specs=[outs] * len(out_shapes) if multi else outs,
+        scratch_shapes=list(scratch),
+        compiler_params=pltpu.CompilerParams(vmem_limit_bytes=limit),
+        cost_estimate=pl.CostEstimate(flops=flops, bytes_accessed=1 << 20, transcendentals=0),
+        name=name,
+    )
+
+
+def pack_kernel(sites, rows, f_ref, o_ref):
+    planes, total = f_ref.shape[0], f_ref.shape[1]
+    block = (rows + 2) * planes
+    for site in range(sites):
+        first = position(site) * rows
+        base = site * block
+        for z in range(planes):
+            for part in range(rows // SUB):
+                tile = f_ref[z, pl.ds(first + part * SUB, SUB), :]
+                o_ref[pl.ds(base + (1 + part * SUB) * planes + z, SUB, stride=planes), :] = tile
+            for idx, row in ((0, first - 1), (rows + 1, first + rows)):
+                if 0 <= row < total:
+                    edge = f_ref[z, pl.ds(row, 1), :]
+                else:
+                    edge = jnp.zeros((1, LANES), jnp.float32)
+                o_ref[pl.ds(base + idx * planes + z, 1), :] = edge
+
+
+def unpack_kernel(sites, rows, ints, r_ref, i_ref, o_ref):
+    core = ints[0]
+    planes = i_ref.shape[0]
+    half = rows // 2
+    for site in range(sites):
+        first = position(site) * rows
+        for part in range(2):
+            who = core if part == 0 else 1 - core
+            base = (site * 2 + part) * half * planes
+            for z in range(planes):
+                for piece in range(half // SUB):
+                    row = pl.multiple_of(first + who * half + piece * SUB, SUB)
+                    tile = r_ref[pl.ds(base + piece * SUB * planes + z, SUB, stride=planes), :]
+                    o_ref[0, z, pl.ds(row, SUB), :] = i_ref[z, pl.ds(row, SUB), :] + tile
+
+
+def shifts(mid, low, high, coefs):
+    depth = mid.shape[0]
+    zp, zm, yp, ym, xp, xm = coefs
+    out = zp * pltpu.roll(mid, depth - 1, 0) + zm * pltpu.roll(mid, 1, 0)
+    out = out + (yp * high + ym * low)
+    return out + (xp * pltpu.roll(mid, LANES - 1, 1) + xm * pltpu.roll(mid, 1, 1))
+
+
+def prepare_coefs(coef_ref, row, c_ref, p_ref, dest, wrap, steps):
+    coupling = coef_ref[row, 0]
+    depth = coupling.shape[0]
+    z = lax.broadcasted_iota(jnp.int32, coupling.shape, 0)
+    x = lax.broadcasted_iota(jnp.int32, coupling.shape, 1)
+    for k in range(3):
+        advect = coupling * coef_ref[row, 1 + k]
+        plus, minus = coupling - advect, coupling + advect
+        if k == 0:
+            plus = jnp.where(z == depth - 1, 0.0, plus)
+            minus = jnp.where(z == 0, 0.0, minus)
+        if k == 2:
+            plus = jnp.where(x == LANES - 1, 0.0, plus)
+            minus = jnp.where(x == 0, 0.0, minus)
+        c_ref[dest, 2 * k] = plus
+        c_ref[dest, 2 * k + 1] = minus
+    inv = 1.0 / (1.0 + 6.0 * coupling)
+    c_ref[dest, 6] = inv
+    powers = [inv]
+    for _ in range(steps - 1):
+        powers.append(powers[-1] * inv)
+    scale = wrap / (1.0 - wrap * powers[-1])
+    for n in range(steps):
+        p_ref[dest, n] = scale * powers[n]
+
+
+def apply_rows(lo, count, steps, src, dst, s_ref, c_ref, p_ref, s_off, c_off, first):
+    def row_body(i, carry):
+        r = lo + i
+        coefs = [c_ref[r - c_off, k] for k in range(6)]
+        inv = c_ref[r - c_off, 6]
+        run = None
+        ys = []
+        for n in range(steps):
+            b = s_ref[r - s_off, n]
+            if not first:
+                b = b + shifts(src[r, n], src[r - 1, n], src[r + 1, n], coefs)
+            run = b * inv if run is None else (b + run) * inv
+            ys.append(run)
+        for n in range(steps):
+            dst[r, n] = ys[n] + ys[-1] * p_ref[r - c_off, n]
+        return carry
+
+    lax.fori_loop(0, count, row_body, 0)
+
+
+def first_kernel(rows, steps, ints, floats, *refs):
+    pieces, (coef_ref,) = refs[:12], refs[12:13]
+    x_out, s_out, last_out = refs[13:16]
+    s_ref, c_ref, p_ref, x0, x1, init_ref = refs[16:]
+    core, side = ints[0], ints[1]
+    wrap = floats[0]
+    half = rows // 2
+    own = half * core
+    window = half + 2 * HALO
+    margin = (coef_ref.shape[0] - rows) // 2
+    sub = lax.broadcasted_iota(jnp.int32, (SUB, LANES), 0)
+
+    def coef_body(i, carry):
+        prepare_coefs(coef_ref, own + margin - HALO + i, c_ref, p_ref, i, wrap, steps)
+        return carry
+
+    lax.fori_loop(0, window, coef_body, 0)
+
+    def source_body(i, carry):
+        row = own + margin - HALO + i
+        coefs = [c_ref[i, k] for k in range(6)]
+        base = shifts(coef_ref[row, 4], coef_ref[row - 1, 4], coef_ref[row + 1, 4], coefs)
+        base = base - 6.0 * coef_ref[row, 0] * coef_ref[row, 4]
+        init_ref[i] = base * (1.0 + wrap)
+        return carry
+
+    lax.fori_loop(0, window, source_body, 0)
+
+    for band, offset in ((0, 0), (1, -rows), (2, rows)):
+        for who in range(2):
+            keep, got = pieces[4 * band + 2 * who], pieces[4 * band + 2 * who + 1]
+            parity = core if who == 0 else 1 - core
+            for pair in range((rows + 2) // 2):
+                for h in range(2):
+                    row = offset + 2 * pair + h - 1
+                    if band == 0 and not 0 <= row < rows:
+                        continue
+                    if band == 1 and row >= 0:
+                        continue
+                    if band == 2 and row < rows:
+                        continue
+                    at = row + HALO - own
+                    ok = jnp.logical_and(at >= 0, at < window)
+
+                    @pl.when(ok)
+                    def _():
+                        for i in range(steps // 2):
+                            a, b = keep[i, pair], got[i, pair]
+                            low = jnp.where(side == 0, a, b)
+                            high = jnp.where(side == 0, b, a)
+                            if h == 0:
+                                tile = jnp.where(sub < SUB // 2, low, pltpu.roll(high, SUB // 2, 0))
+                            else:
+                                tile = jnp.where(sub < SUB // 2, pltpu.roll(low, SUB // 2, 0), high)
+                            s_ref[at, 2 * i + parity] = tile + init_ref[at]
+
+    bufs = (x0, x1)
+    for k in range(1, APPS + 1):
+        reach = HALO + 1 - k
+        apply_rows(
+            HALO - reach,
+            half + 2 * reach,
+            steps,
+            bufs[k % 2],
+            bufs[(k + 1) % 2],
+            s_ref,
+            c_ref,
+            p_ref,
+            0,
+            0,
+            k == 1,
+        )
+    final = bufs[(APPS + 1) % 2]
+    reach = HALO + 1 - APPS
+    start = HALO - reach
+
+    def out_body(i, carry):
+        for n in range(steps):
+            x_out[i, n] = final[start + i, n]
+        return carry
+
+    lax.fori_loop(0, half + 2 * reach, out_body, 0)
+
+    def out_source(i, carry):
+        for n in range(steps):
+            s_out[i, n] = s_ref[start + 1 + i, n]
+        last_out[i] = final[start + 1 + i, steps - 1]
+        return carry
+
+    lax.fori_loop(0, half + 2 * (reach - 1), out_source, 0)
+
+
+def second_kernel(rows, steps, ints, floats, x_ref, s_ref, last_ref, other_ref, coef_ref, *refs):
+    keep_near, keep_far, send_near, send_far = refs[:4]
+    c_ref, p_ref, s0_ref, xa, xb = refs[4:]
+    core, side = ints[0], ints[1]
+    wrap = floats[0]
+    half = rows // 2
+    own = half * core
+    reach = HALO - APPS
+    window = half + 2 * reach
+    margin = (coef_ref.shape[0] - rows) // 2
+
+    def coef_body(i, carry):
+        prepare_coefs(coef_ref, own + margin - reach + i, c_ref, p_ref, i, wrap, steps)
+        for n in range(steps):
+            s0_ref[i, n] = s_ref[i, n]
+        s0_ref[i, 0] = s_ref[i, 0] - (0.5 * wrap) * (last_ref[i] - other_ref[i])
+        return carry
+
+    lax.fori_loop(0, window, coef_body, 0)
+
+    bufs = [x_ref, xa]
+    src, dst = x_ref, xa
+    for k in range(1, APPS + 1):
+        left = reach + 1 - k
+        apply_rows(
+            1 + reach - left, half + 2 * left, steps, src, dst, s0_ref, c_ref, p_ref, 1, 1, False
+        )
+        src, dst = dst, (xb if dst is xa else xa)
+    sub = lax.broadcasted_iota(jnp.int32, (SUB, LANES), 0)
+    for pair in range(half // 2):
+        for i in range(steps // 2):
+            for to_core, near, far in ((0, keep_near, keep_far), (1, send_near, send_far)):
+                parity = core if to_core == 0 else 1 - core
+                a = src[1 + reach + 2 * pair, 2 * i + parity]
+                b = src[1 + reach + 2 * pair + 1, 2 * i + parity]
+                low = jnp.where(sub < SUB // 2, a, pltpu.roll(b, SUB // 2, 0))
+                high = jnp.where(sub < SUB // 2, pltpu.roll(a, SUB // 2, 0), b)
+                near[i, pair] = jnp.where(side == 0, low, high)
+                far[i, pair] = jnp.where(side == 0, high, low)
+
+
+def banded_body(forcing, initial, coupling, velocity):
+    f32 = jnp.float32
+    groups = lax.axis_size("tm")
+    sites = groups // 2
+    steps = groups // 2
+    planes, height, width = initial.shape
+    rows = height // sites
+    half = rows // 2
+    time_index = lax.axis_index("tm")
+    side = lax.axis_index("space")
+    core = time_index % 2
+    site = time_index // 2
+    place = position(site)
+    root = math.sqrt(wrap_alpha)
+    wrap = jnp.where(side == 0, root, -root).astype(f32)
+    ints = jnp.stack([core, side]).astype(jnp.int32)
+    floats = wrap[None]
+
+    same_core = [[2 * i + c for i in range(sites)] for c in range(2)]
+    cores = [(i, i ^ 1) for i in range(groups)]
+    sides = [(0, 1), (1, 0)]
+    by_place = {position(q): q for q in range(sites)}
+    ahead = [
+        (2 * by_place[p] + c, 2 * by_place[p + 1] + c) for p in range(sites - 1) for c in range(2)
+    ]
+    back = [(b, a) for a, b in ahead]
+
+    margin = HALO + 1
+    margin = -(-(2 * margin + rows) // SUB) * SUB
+    margin = (margin - rows) // 2
+    fields = jnp.concatenate([coupling[None], velocity, initial[None]], axis=0)
+    padded = jnp.pad(fields, ((0, 0), (0, 0), (margin, margin), (0, 0)))
+    mine = lax.dynamic_slice_in_dim(padded, place * rows, rows + 2 * margin, axis=2)
+    theirs = lax.ppermute(mine, "space", sides)
+
+    packed = vmem_call(
+        functools.partial(pack_kernel, sites, rows),
+        jax.ShapeDtypeStruct((sites * (rows + 2) * planes, width), f32),
+        1,
+        name="pack",
+    )(forcing[0])
+    packed = packed.reshape(sites, (rows + 2) // 2, 2 * planes, width)
+    bands = lax.all_to_all(
+        packed, "tm", split_axis=0, concat_axis=0, tiled=True, axis_index_groups=same_core
+    )
+    near, far = bands[: steps // 2], bands[steps // 2 :]
+    keep = near + wrap * far
+    send = near - wrap * far
+    got = lax.ppermute(send, "space", sides)
+
+    pieces = []
+    for keep_b, got_b in (
+        (keep, got),
+        (lax.ppermute(keep, "tm", ahead), lax.ppermute(got, "tm", ahead)),
+        (lax.ppermute(keep, "tm", back), lax.ppermute(got, "tm", back)),
+    ):
+        pieces += [keep_b, got_b, lax.ppermute(keep_b, "tm", cores), lax.ppermute(got_b, "tm", cores)]
+
+    halves = jnp.where(side == 0, mine, theirs), jnp.where(side == 0, theirs, mine)
+    coefs = jnp.concatenate(halves, axis=1).transpose(2, 0, 1, 3)
+
+    depth = 2 * planes
+    window = half + 2 * HALO
+    reach = HALO + 1 - APPS
+    limit = 48 * 1024 * 1024
+    tile = (depth, width)
+    x_mid, s_mid, last = vmem_call(
+        functools.partial(first_kernel, rows, steps),
+        [
+            jax.ShapeDtypeStruct((half + 2 * reach, steps) + tile, f32),
+            jax.ShapeDtypeStruct((half + 2 * reach - 2, steps) + tile, f32),
+            jax.ShapeDtypeStruct((half + 2 * reach - 2,) + tile, f32),
+        ],
+        13,
+        scratch=[
+            pltpu.VMEM((window, steps) + tile, f32),
+            pltpu.VMEM((window, 7) + tile, f32),
+            pltpu.VMEM((window, steps) + tile, f32),
+            pltpu.VMEM((window, steps) + tile, f32),
+            pltpu.VMEM((window, steps) + tile, f32),
+            pltpu.VMEM((window,) + tile, f32),
+        ],
+        n_smem=2,
+        flops=20_000_000,
+        limit=limit,
+        name="first",
+    )(ints, floats, *pieces, coefs)
+    other = lax.ppermute(last, "space", sides)
+    quarter = jax.ShapeDtypeStruct((steps // 2, half // 2, depth, width), f32)
+    keep_near, keep_far, send_near, send_far = vmem_call(
+        functools.partial(second_kernel, rows, steps),
+        [quarter] * 4,
+        5,
+        scratch=[
+            pltpu.VMEM((half + 2 * reach - 2, 7) + tile, f32),
+            pltpu.VMEM((half + 2 * reach - 2, steps) + tile, f32),
+            pltpu.VMEM((half + 2 * reach - 2, steps) + tile, f32),
+            pltpu.VMEM((half + 2 * reach, steps) + tile, f32),
+            pltpu.VMEM((half + 2 * reach, steps) + tile, f32),
+        ],
+        n_smem=2,
+        flops=10_000_000,
+        limit=limit,
+        name="second",
+    )(ints, floats, x_mid, s_mid, last, other, coefs)
+
+    got_near = lax.ppermute(send_near, "tm", cores)
+    got_far = lax.ppermute(send_far, "tm", cores)
+    mate_near = lax.ppermute(keep_far, "space", sides)
+    mate_far = lax.ppermute(got_far, "space", sides)
+    ours = jnp.stack([keep_near, got_near], axis=1)
+    mates = jnp.stack([mate_near, mate_far], axis=1)
+    early = 0.5 * (ours + mates)
+    late = (0.5 / (wrap)) * (ours - mates)
+    result = jnp.concatenate([early, late], axis=0)
+    spread = lax.all_to_all(
+        result, "tm", split_axis=0, concat_axis=0, tiled=True, axis_index_groups=same_core
+    )
+    return vmem_call(
+        functools.partial(unpack_kernel, sites, rows),
+        jax.ShapeDtypeStruct((1, planes, height, width), f32),
+        2,
+        n_smem=1,
+        name="unpack",
+    )(ints, spread.reshape(-1, width), initial)
 
 
 def passed_along(array, axis, by):
@@ -81,7 +458,7 @@
     return jnp.stack([value_re, value_im])
 
 
-def body(forcing, initial, coupling, velocity):
+def general_body(forcing, initial, coupling, velocity):
     local_steps = forcing.shape[0]
     groups = lax.axis_size("tm")
     total_steps = local_steps * groups
@@ -134,6 +511,23 @@
     return iterate
 
 
+def body(forcing, initial, coupling, velocity):
+    groups = lax.axis_size("tm")
+    planes, height, width = initial.shape
+    fits = (
+        ITERS == 2
+        and forcing.shape[0] == 1
+        and groups % 4 == 0
+        and lax.axis_size("space") == 2
+        and 2 * planes == SUB
+        and width == LANES
+        and height % (groups * SUB) == 0
+        and height // (groups // 2) + 1 >= HALO
+    )
+    plan = banded_body if fits else general_body
+    return plan(forcing, initial, coupling, velocity)
+
+
 def solution(mesh):
     return jax.shard_map(
         body,

time: 319 us -> 114 us (0.36)
  blocking collectives: 111 us -> 15.2 us
  waiting for transfers between devices: 113 us -> 18.7 us
  Pallas kernels: 0 us -> 51.4 us
  starting transfers between devices: 61.2 us -> 26.1 us
  other arithmetic: 23.6 us -> 1.54 us
  local copies, waits for them, and re-layouts: 4.47 us -> 0.88 us
  matrix products: 3.5 us -> 0 us
    all_to_all x7 -> x1, blocking collectives: 111 us -> 15.2 us  [banded_body(): lax.all_to_all(result, 'tm', split_axis=0, concat_axis=0, tiled=True, axi...]
    ppermute x38 -> x17, waiting for transfers between devices: 99.2 us -> 12.1 us  [the longest x1 3.33 us: banded_body(): other = lax.ppermute(last, 'space', sides)]
    pallas_call x0 -> x4, Pallas kernels: none -> 51.4 us  [the longest x1 32.7 us: banded_body(): vmem_call(functools.partial(first_kernel, rows, steps), [jax.ShapeDtypeSt...]
    ppermute x38 -> x17, starting transfers between devices: 57.6 us -> 18.7 us  [the longest x1 4.55 us: banded_body(): lax.ppermute(got, 'tm', ahead)]
    add x18 -> x0, other arithmetic: 9.67 us -> none  [the longest x16 8.91 us: coupled(): total + (coupling - advect[2]) * extended[..., 1:-1, 1:-1, 2:]]
    concatenate x18 -> x2, other arithmetic: 8.58 us -> 0.51 us  [the longest x1 0.49 us: banded_body(): fields = jnp.concatenate([coupling[None], velocity, initial[None]], axis=0)]
    all_to_all x1, waiting for transfers between devices: 14.1 us -> 6.64 us  [banded_body(): lax.all_to_all(packed, 'tm', split_axis=0, concat_axis=0, tiled=True, axi...]
    all_to_all x1, starting transfers between devices: 3.57 us -> 7.41 us  [banded_body(): lax.all_to_all(packed, 'tm', split_axis=0, concat_axis=0, tiled=True, axi...]
  transfers between devices with their start and end apart: 39 -> 18, of which waited for: 36 -> 8; matrix products, arithmetic and copies ran while one was open for 1% -> 2% of each run, Pallas kernels for 0% -> 0%
where the time goes in v1:
time: 114 us
  Pallas kernels  51.4 us (45%)
  starting transfers between devices  26.1 us (23%)
  waiting for transfers between devices  18.7 us (16%)
  blocking collectives  15.2 us (13%)
  other arithmetic  1.54 us (1%)
    pallas_call x1, Pallas kernels, banded_body(): vmem_call(functools.partial(first_kernel, rows, steps), [jax.ShapeDtypeSt...  32.7 us
    all_to_all x1, blocking collectives, banded_body(): lax.all_to_all(result, 'tm', split_axis=0, concat_axis=0, tiled=True, axi...  15.2 us
    pallas_call x1, Pallas kernels, banded_body(): vmem_call(functools.partial(second_kernel, rows, steps), [quarter] * 4, 5...  15.1 us
    all_to_all x1, starting transfers between devices, banded_body(): lax.all_to_all(packed, 'tm', split_axis=0, concat_axis=0, tiled=True, axi...  7.41 us
    all_to_all x1, waiting for transfers between devices, banded_body(): lax.all_to_all(packed, 'tm', split_axis=0, concat_axis=0, tiled=True, axi...  6.64 us
    ppermute x1, starting transfers between devices, banded_body(): lax.ppermute(got, 'tm', ahead)  4.55 us
    ppermute x1, waiting for transfers between devices, banded_body(): other = lax.ppermute(last, 'space', sides)  3.33 us
    ppermute x1, starting transfers between devices, banded_body(): lax.ppermute(keep, 'tm', ahead)  3.32 us
  transfers between devices with their start and end apart: 18, of which 8 were waited for; matrix products, arithmetic and copies ran while one was open for 2% of the time, Pallas kernels for 0%

profile of v1, /device:TPU:0, one launch (start us, length us, event | category | flops | bytes accessed | tf_op | source)
XLA Modules:
  0.0 114.1 jit_solution(14310635687954300777)
XLA Ops:
  0.0 0.0 copy-start.2
  0.0 1.8 %pack.1 = f32[576,128]{1,0:T(8,128)} custom-call(f32[4,128,128]{2,1,0:T(8,128)} %bitcast.19), custom_call_target="tpu_custom_call" | custom-call | bytes 1048576 | tf_op jit(solution)/shard_map/pack/pallas_call | solution.py:300
  1.8 0.0 copy-start.1
  1.8 0.0 copy-start.3
  1.8 7.4 %all-to-all-start = ((f32[8,9,8,128]{3,2,1,0:T(8,128)}), f32[8,9,8,128]{3,2,1,0:T(8,128)S(1)}, u32[]{:S(2)}, u32[]{:S(2)}) async-start(f32[8,9,8,128]{3,2,1,0:T(8,128)} %bitcast.17), calls=%async_computation | async-start | bytes 589824 | tf_op jit(solution)/shard_map/all_to_all | solution.py:307
  9.2 0.0 copy-done.2
  9.2 0.5 copy.11
  9.7 0.0 copy-done.1
  9.7 0.0 copy-done.3
  9.8 0.3 copy_bitcast_fusion
  10.1 0.5 fusion.2
  10.6 1.6 %collective-permute-start.11 = (f32[5,4,56,128]{3,1,0,2:T(4,128)S(1)}, f32[5,4,56,128]{3,1,0,2:T(4,128)S(1)}, u32[]{:S(2)}, u32[]{:S(2)}) collective-permute-start(f32[5,4,56,128]{3,1,0,2:T(4,128)S(1)} %fusion.2), channel_id=1, source_target_pairs={{0,1},{1,0},{2,3},{3,2},{4,5},{5,4},{6,7},{7,6},{8,9},{9,8},{10,11... | collective-permute-start | bytes 1720328 | tf_op jit(solution)/shard_map/ppermute | solution.py:298
  12.2 6.6 %all-to-all-done = f32[8,9,8,128]{3,2,1,0:T(8,128)S(1)} async-done(((f32[8,9,8,128]{3,2,1,0:T(8,128)}), f32[8,9,8,128]{3,2,1,0:T(8,128)S(1)}, u32[]{:S(2)}, u32[]{:S(2)}) %all-to-all-start) | async-done | bytes 294944 | tf_op jit(solution)/shard_map/all_to_all | solution.py:307
  18.8 1.6 %collective-permute-start = (f32[4,9,8,128]{3,2,1,0:T(8,128)S(1)}, f32[4,9,8,128]{3,2,1,0:T(8,128)S(1)}, u32[]{:S(2)}, u32[]{:S(2)}) collective-permute-start(f32[4,9,8,128]{3,2,1,0:T(8,128)S(1)} %get-tuple-element.21), channel_id=1, source_target_pairs={{0,1},{1,0},{2,3},{3,2},{4,5},{5,4},{6,7},{7,6},{8,9},{9,8},{10,11... | collective-permute-start | bytes 442376 | tf_op jit(solution)/shard_map/ppermute | solution.py:313
  20.4 3.3 %collective-permute-start.3 = (f32[4,9,8,128]{3,2,1,0:T(8,128)S(1)}, f32[4,9,8,128]{3,2,1,0:T(8,128)S(1)}, u32[]{:S(2)}, u32[]{:S(2)}) collective-permute-start(f32[4,9,8,128]{3,2,1,0:T(8,128)S(1)} %get-tuple-element.22.refs_0_), channel_id=1, source_target_pairs={{0,4},{2,6},{4,12},{6,14},{12,8},{14,10},{8,16},{10,18},{16,20},{1... | collective-permute-start | bytes 442376 | tf_op jit(solution)/shard_map/ppermute | solution.py:318
  23.8 1.3 %collective-permute-start.7 = (f32[4,9,8,128]{3,2,1,0:T(8,128)S(1)}, f32[4,9,8,128]{3,2,1,0:T(8,128)S(1)}, u32[]{:S(2)}, u32[]{:S(2)}) collective-permute-start(f32[4,9,8,128]{3,2,1,0:T(8,128)S(1)} %get-tuple-element.22.refs_0_), channel_id=1, source_target_pairs={{4,0},{6,2},{12,4},{14,6},{8,12},{10,14},{16,8},{18,10},{20,16},{2... | collective-permute-start | bytes 442376 | tf_op jit(solution)/shard_map/ppermute | solution.py:319
  25.1 0.1 collective-permute-start.1
  25.1 3.1 %collective-permute-done.refs_1_ = f32[4,9,8,128]{3,2,1,0:T(8,128)S(1)} collective-permute-done((f32[4,9,8,128]{3,2,1,0:T(8,128)S(1)}, f32[4,9,8,128]{3,2,1,0:T(8,128)S(1)}, u32[]{:S(2)}, u32[]{:S(2)}) %collective-permute-start) | collective-permute-done | bytes 147488 | tf_op jit(solution)/shard_map/ppermute | solution.py:313
  28.3 1.3 %collective-permute-start.8 = (f32[4,9,8,128]{3,2,1,0:T(8,128)S(1)}, f32[4,9,8,128]{3,2,1,0:T(8,128)S(1)}, u32[]{:S(2)}, u32[]{:S(2)}) collective-permute-start(f32[4,9,8,128]{3,2,1,0:T(8,128)S(1)} %collective-permute-done.refs_1_), channel_id=1, source_target_pairs={{4,0},{6,2},{12,4},{14,6},{8,12},{10,14},{16,8},{18,10},{20,16},{2... | collective-permute-start | bytes 442376 | tf_op jit(solution)/shard_map/ppermute | solution.py:319
  29.5 0.0 collective-permute-done.11
  29.6 4.6 %collective-permute-start.4 = (f32[4,9,8,128]{3,2,1,0:T(8,128)S(1)}, f32[4,9,8,128]{3,2,1,0:T(8,128)S(1)}, u32[]{:S(2)}, u32[]{:S(2)}) collective-permute-start(f32[4,9,8,128]{3,2,1,0:T(8,128)S(1)} %collective-permute-done.refs_1_), channel_id=1, source_target_pairs={{0,4},{2,6},{4,12},{6,14},{12,8},{14,10},{8,16},{10,18},{16,20},{1... | collective-permute-start | bytes 442376 | tf_op jit(solution)/shard_map/ppermute | solution.py:318
  34.1 0.1 pad_add_fusion.ints
  34.2 0.0 copy-start
  34.2 0.0 collective-permute-done.3.refs_4_
  34.2 0.0 collective-permute-start.2
  34.2 0.0 collective-permute-done.7.refs_8_
  34.3 0.5 collective-permute-start.5
  34.7 0.0 collective-permute-done.1.refs_2_
  34.7 0.1 collective-permute-start.9
  34.8 0.4 collective-permute-done.8.refs_9_
  35.3 0.0 collective-permute-start.10
  35.3 1.5 %collective-permute-done.4.refs_5_ = f32[4,9,8,128]{3,2,1,0:T(8,128)S(1)} collective-permute-done((f32[4,9,8,128]{3,2,1,0:T(8,128)S(1)}, f32[4,9,8,128]{3,2,1,0:T(8,128)S(1)}, u32[]{:S(2)}, u32[]{:S(2)}) %collective-permute-start.4) | collective-permute-done | bytes 147488 | tf_op jit(solution)/shard_map/ppermute | solution.py:318
  36.8 0.0 collective-permute-start.6
  36.8 0.7 broadcast_select_fusion.1
  37.5 0.2 maximum_bitcast_fusion.refs_12_.coef_ref
  37.7 0.0 collective-permute-done.5.refs_6_
  37.7 0.0 collective-permute-done.9.refs_10_
  37.7 0.0 collective-permute-done.2.refs_3_
  37.7 0.0 collective-permute-done.10.refs_11_
  37.7 0.4 collective-permute-done.6.refs_7_
  38.1 32.7 %first.1 = (f32[26,8,8,128]{3,2,1,0:T(8,128)S(1)}, f32[24,8,8,128]{3,2,1,0:T(8,128)S(1)}, f32[24,8,128]{2,1,0:T(8,128)S(1)}) custom-call(s32[2]{0:T(128)S(1)} %pad_add_fusion.ints, f32[1]{0:T(128)} %bitcast.2.floats, f32[4,9,8,128]{3,2,1,0:T(8,128)S(1)} %get-tuple-element.22.refs_0_, f32[4,9,8,128]{3,2,1,0:T(8,128)S(1)} %collective-permute-done.refs_1_, ...), custom_call_target="tpu_custom_call" | custom-call | flops 20000000 | bytes 1048576 | tf_op jit(solution)/shard_map/first/pallas_call | solution.py:331
  70.9 1.6 %collective-permute-start.12 = (f32[24,8,128]{2,1,0:T(8,128)S(1)}, f32[24,8,128]{2,1,0:T(8,128)S(1)}, u32[]{:S(2)}, u32[]{:S(2)}) collective-permute-start(f32[24,8,128]{2,1,0:T(8,128)S(1)} %get-tuple-element.14.last_ref), channel_id=1, source_target_pairs={{0,1},{1,0},{2,3},{3,2},{4,5},{5,4},{6,7},{7,6},{8,9},{9,8},{10,11... | collective-permute-start | bytes 294920 | tf_op jit(solution)/shard_map/ppermute | solution.py:352
  72.5 3.3 %collective-permute-done.12.other_ref = f32[24,8,128]{2,1,0:T(8,128)S(1)} collective-permute-done((f32[24,8,128]{2,1,0:T(8,128)S(1)}, f32[24,8,128]{2,1,0:T(8,128)S(1)}, u32[]{:S(2)}, u32[]{:S(2)}) %collective-permute-start.12) | collective-permute-done | bytes 98336 | tf_op jit(solution)/shard_map/ppermute | solution.py:352
  75.8 0.0 copy-done
  75.8 15.1 %second.1 = (f32[4,4,8,128]{3,2,1,0:T(8,128)S(1)}, f32[4,4,8,128]{3,2,1,0:T(8,128)S(1)}, f32[4,4,8,128]{3,2,1,0:T(8,128)S(1)}, f32[4,4,8,128]{3,2,1,0:T(8,128)S(1)}) custom-call(s32[2]{0:T(128)S(1)} %pad_add_fusion.ints, f32[1]{0:T(128)} %bitcast.2.floats, f32[26,8,8,128]{3,2,1,0:T(8,128)S(1)} %get-tuple-element.12.x_ref, ...), custom_call_target="tpu_custom_call" | custom-call | flops 10000000 | bytes 1048576 | tf_op jit(solution)/shard_map/second/pallas_call | solution.py:354
  90.9 0.1 collective-permute-start.15
  90.9 1.6 %collective-permute-start.14 = (f32[4,4,8,128]{3,2,1,0:T(8,128)S(1)}, f32[4,4,8,128]{3,2,1,0:T(8,128)S(1)}, u32[]{:S(2)}, u32[]{:S(2)}) collective-permute-start(f32[4,4,8,128]{3,2,1,0:T(8,128)S(1)} %get-tuple-element.17), channel_id=1, source_target_pairs={{0,1},{1,0},{2,3},{3,2},{4,5},{5,4},{6,7},{7,6},{8,9},{9,8},{10,11... | collective-permute-start | bytes 196616 | tf_op jit(solution)/shard_map/ppermute | solution.py:373
  92.5 0.2 collective-permute-start.13
  92.7 0.0 collective-permute-done.15
  92.7 1.0 collective-permute-start.16
  93.8 1.7 %collective-permute-done.14 = f32[4,4,8,128]{3,2,1,0:T(8,128)S(1)} collective-permute-done((f32[4,4,8,128]{3,2,1,0:T(8,128)S(1)}, f32[4,4,8,128]{3,2,1,0:T(8,128)S(1)}, u32[]{:S(2)}, u32[]{:S(2)}) %collective-permute-start.14) | collective-permute-done | bytes 65568 | tf_op jit(solution)/shard_map/ppermute | solution.py:373
  95.4 0.0 collective-permute-done.13
  95.4 1.6 %collective-permute-done.16 = f32[4,4,8,128]{3,2,1,0:T(8,128)S(1)} collective-permute-done((f32[4,4,8,128]{3,2,1,0:T(8,128)S(1)}, f32[4,4,8,128]{3,2,1,0:T(8,128)S(1)}, u32[]{:S(2)}, u32[]{:S(2)}) %collective-permute-start.16) | collective-permute-done | bytes 65568 | tf_op jit(solution)/shard_map/ppermute | solution.py:374
  97.1 15.2 %all_to_all.10 = f32[8,2,4,8,128]{4,3,2,1,0:T(8,128)} all-to-all(f32[8,2,4,8,128]{4,3,2,1,0:T(8,128)S(1)} %copy.12), channel_id=1, replica_groups={{0,4,8,12,16,20,24,28},{2,6,10,14,18,22,26,30},{1,5,9,13,17,21,25,29},{..., dimensions={0} | all-to-all | bytes 524288 | tf_op jit(solution)/shard_map/all_to_all | solution.py:380
  112.3 1.8 %unpack.1 = f32[1,4,128,128]{3,2,1,0:T(8,128)} custom-call(s32[2]{0:T(128)} %copy-done, f32[512,128]{1,0:T(8,128)} %bitcast.18, f32[4,128,128]{2,1,0:T(8,128)} %i_ref.1), custom_call_target="tpu_custom_call" | custom-call | bytes 1048576 | tf_op jit(solution)/shard_map/unpack/pallas_call | solution.py:383
  (4 shorter events, 0.1 us)
Async XLA Ops:
  0.0 9.2 %copy-start.2 = (f32[3,4,128,128]{3,2,1,0:T(8,128)S(1)}, f32[3,4,128,128]{3,2,1,0:T(8,128)}, u32[]{:S(2)}) copy-start(f32[3,4,128,128]{3,2,1,0:T(8,128)} %param.7) | copy-start | bytes 2359300
  1.8 7.9 %copy-start.1 = (f32[4,128,128]{2,1,0:T(8,128)S(1)}, f32[4,128,128]{2,1,0:T(8,128)}, u32[]{:S(2)}) copy-start(f32[4,128,128]{2,1,0:T(8,128)} %i_ref.1) | copy-start | bytes 786436
  1.8 8.0 %copy-start.3 = (f32[4,128,128]{2,1,0:T(8,128)S(1)}, f32[4,128,128]{2,1,0:T(8,128)}, u32[]{:S(2)}) copy-start(f32[4,128,128]{2,1,0:T(8,128)} %param.6) | copy-start | bytes 786436
  1.8 17.0 %all-to-all-start = ((f32[8,9,8,128]{3,2,1,0:T(8,128)}), f32[8,9,8,128]{3,2,1,0:T(8,128)S(1)}, u32[]{:S(2)}, u32[]{:S(2)}) async-start(f32[8,9,8,128]{3,2,1,0:T(8,128)} %bitcast.17), calls=%async_computation | async-start | bytes 589824 | tf_op jit(solution)/shard_map/all_to_all | solution.py:307
  10.6 19.0 %collective-permute-start.11 = (f32[5,4,56,128]{3,1,0,2:T(4,128)S(1)}, f32[5,4,56,128]{3,1,0,2:T(4,128)S(1)}, u32[]{:S(2)}, u32[]{:S(2)}) collective-permute-start(f32[5,4,56,128]{3,1,0,2:T(4,128)S(1)} %fusion.2), channel_id=1, source_target_pairs={{0,1},{1,0},{2,3},{3,2},{4,5},{5,4},{6,7},{7,6},{8,9},{9,8},{10,11... | collective-permute-start | bytes 1720328 | tf_op jit(solution)/shard_map/ppermute | solution.py:298
  18.8 9.4 %collective-permute-start = (f32[4,9,8,128]{3,2,1,0:T(8,128)S(1)}, f32[4,9,8,128]{3,2,1,0:T(8,128)S(1)}, u32[]{:S(2)}, u32[]{:S(2)}) collective-permute-start(f32[4,9,8,128]{3,2,1,0:T(8,128)S(1)} %get-tuple-element.21), channel_id=1, source_target_pairs={{0,1},{1,0},{2,3},{3,2},{4,5},{5,4},{6,7},{7,6},{8,9},{9,8},{10,11... | collective-permute-start | bytes 442376 | tf_op jit(solution)/shard_map/ppermute | solution.py:313
  20.4 13.8 %collective-permute-start.3 = (f32[4,9,8,128]{3,2,1,0:T(8,128)S(1)}, f32[4,9,8,128]{3,2,1,0:T(8,128)S(1)}, u32[]{:S(2)}, u32[]{:S(2)}) collective-permute-start(f32[4,9,8,128]{3,2,1,0:T(8,128)S(1)} %get-tuple-element.22.refs_0_), channel_id=1, source_target_pairs={{0,4},{2,6},{4,12},{6,14},{12,8},{14,10},{8,16},{10,18},{16,20},{1... | collective-permute-start | bytes 442376 | tf_op jit(solution)/shard_map/ppermute | solution.py:318
  23.8 10.5 %collective-permute-start.7 = (f32[4,9,8,128]{3,2,1,0:T(8,128)S(1)}, f32[4,9,8,128]{3,2,1,0:T(8,128)S(1)}, u32[]{:S(2)}, u32[]{:S(2)}) collective-permute-start(f32[4,9,8,128]{3,2,1,0:T(8,128)S(1)} %get-tuple-element.22.refs_0_), channel_id=1, source_target_pairs={{4,0},{6,2},{12,4},{14,6},{8,12},{10,14},{16,8},{18,10},{20,16},{2... | collective-permute-start | bytes 442376 | tf_op jit(solution)/shard_map/ppermute | solution.py:319
  25.1 9.7 %collective-permute-start.1 = (f32[4,9,8,128]{3,2,1,0:T(8,128)S(1)}, f32[4,9,8,128]{3,2,1,0:T(8,128)S(1)}, u32[]{:S(2)}, u32[]{:S(2)}) collective-permute-start(f32[4,9,8,128]{3,2,1,0:T(8,128)S(1)} %get-tuple-element.22.refs_0_), channel_id=1, source_target_pairs={{0,2},{2,0},{4,6},{6,4},{8,10},{10,8},{12,14},{14,12},{16,18},{18,... | collective-permute-start | bytes 442376 | tf_op jit(solution)/shard_map/ppermute | solution.py:321
  28.3 7.0 %collective-permute-start.8 = (f32[4,9,8,128]{3,2,1,0:T(8,128)S(1)}, f32[4,9,8,128]{3,2,1,0:T(8,128)S(1)}, u32[]{:S(2)}, u32[]{:S(2)}) collective-permute-start(f32[4,9,8,128]{3,2,1,0:T(8,128)S(1)} %collective-permute-done.refs_1_), channel_id=1, source_target_pairs={{4,0},{6,2},{12,4},{14,6},{8,12},{10,14},{16,8},{18,10},{20,16},{2... | collective-permute-start | bytes 442376 | tf_op jit(solution)/shard_map/ppermute | solution.py:319
  29.6 7.2 %collective-permute-start.4 = (f32[4,9,8,128]{3,2,1,0:T(8,128)S(1)}, f32[4,9,8,128]{3,2,1,0:T(8,128)S(1)}, u32[]{:S(2)}, u32[]{:S(2)}) collective-permute-start(f32[4,9,8,128]{3,2,1,0:T(8,128)S(1)} %collective-permute-done.refs_1_), channel_id=1, source_target_pairs={{0,4},{2,6},{4,12},{6,14},{12,8},{14,10},{8,16},{10,18},{16,20},{1... | collective-permute-start | bytes 442376 | tf_op jit(solution)/shard_map/ppermute | solution.py:318
  34.2 41.6 %copy-start = (s32[2]{0:T(128)}, s32[2]{0:T(128)S(1)}, u32[]{:S(2)}) copy-start(s32[2]{0:T(128)S(1)} %pad_add_fusion.ints) | copy-start | bytes 28
  34.2 3.5 %collective-permute-start.2 = (f32[4,9,8,128]{3,2,1,0:T(8,128)S(1)}, f32[4,9,8,128]{3,2,1,0:T(8,128)S(1)}, u32[]{:S(2)}, u32[]{:S(2)}) collective-permute-start(f32[4,9,8,128]{3,2,1,0:T(8,128)S(1)} %collective-permute-done.refs_1_), channel_id=1, source_target_pairs={{0,2},{2,0},{4,6},{6,4},{8,10},{10,8},{12,14},{14,12},{16,18},{18,... | collective-permute-start | bytes 442376 | tf_op jit(solution)/shard_map/ppermute | solution.py:321
  34.3 3.4 %collective-permute-start.5 = (f32[4,9,8,128]{3,2,1,0:T(8,128)S(1)}, f32[4,9,8,128]{3,2,1,0:T(8,128)S(1)}, u32[]{:S(2)}, u32[]{:S(2)}) collective-permute-start(f32[4,9,8,128]{3,2,1,0:T(8,128)S(1)} %collective-permute-done.3.refs_4_), channel_id=1, source_target_pairs={{0,2},{2,0},{4,6},{6,4},{8,10},{10,8},{12,14},{14,12},{16,18},{18,... | collective-permute-start | bytes 442376 | tf_op jit(solution)/shard_map/ppermute | solution.py:321
  34.7 3.0 %collective-permute-start.9 = (f32[4,9,8,128]{3,2,1,0:T(8,128)S(1)}, f32[4,9,8,128]{3,2,1,0:T(8,128)S(1)}, u32[]{:S(2)}, u32[]{:S(2)}) collective-permute-start(f32[4,9,8,128]{3,2,1,0:T(8,128)S(1)} %collective-permute-done.7.refs_8_), channel_id=1, source_target_pairs={{0,2},{2,0},{4,6},{6,4},{8,10},{10,8},{12,14},{14,12},{16,18},{18,... | collective-permute-start | bytes 442376 | tf_op jit(solution)/shard_map/ppermute | solution.py:321
  35.3 2.4 %collective-permute-start.10 = (f32[4,9,8,128]{3,2,1,0:T(8,128)S(1)}, f32[4,9,8,128]{3,2,1,0:T(8,128)S(1)}, u32[]{:S(2)}, u32[]{:S(2)}) collective-permute-start(f32[4,9,8,128]{3,2,1,0:T(8,128)S(1)} %collective-permute-done.8.refs_9_), channel_id=1, source_target_pairs={{0,2},{2,0},{4,6},{6,4},{8,10},{10,8},{12,14},{14,12},{16,18},{18,... | collective-permute-start | bytes 442376 | tf_op jit(solution)/shard_map/ppermute | solution.py:321
  36.8 1.4 %collective-permute-start.6 = (f32[4,9,8,128]{3,2,1,0:T(8,128)S(1)}, f32[4,9,8,128]{3,2,1,0:T(8,128)S(1)}, u32[]{:S(2)}, u32[]{:S(2)}) collective-permute-start(f32[4,9,8,128]{3,2,1,0:T(8,128)S(1)} %collective-permute-done.4.refs_5_), channel_id=1, source_target_pairs={{0,2},{2,0},{4,6},{6,4},{8,10},{10,8},{12,14},{14,12},{16,18},{18,... | collective-permute-start | bytes 442376 | tf_op jit(solution)/shard_map/ppermute | solution.py:321
  70.9 4.9 %collective-permute-start.12 = (f32[24,8,128]{2,1,0:T(8,128)S(1)}, f32[24,8,128]{2,1,0:T(8,128)S(1)}, u32[]{:S(2)}, u32[]{:S(2)}) collective-permute-start(f32[24,8,128]{2,1,0:T(8,128)S(1)} %get-tuple-element.14.last_ref), channel_id=1, source_target_pairs={{0,1},{1,0},{2,3},{3,2},{4,5},{5,4},{6,7},{7,6},{8,9},{9,8},{10,11... | collective-permute-start | bytes 294920 | tf_op jit(solution)/shard_map/ppermute | solution.py:352
  90.9 1.8 %collective-permute-start.15 = (f32[4,4,8,128]{3,2,1,0:T(8,128)S(1)}, f32[4,4,8,128]{3,2,1,0:T(8,128)S(1)}, u32[]{:S(2)}, u32[]{:S(2)}) collective-permute-start(f32[4,4,8,128]{3,2,1,0:T(8,128)S(1)} %get-tuple-element.18), channel_id=1, source_target_pairs={{0,2},{2,0},{4,6},{6,4},{8,10},{10,8},{12,14},{14,12},{16,18},{18,... | collective-permute-start | bytes 196616 | tf_op jit(solution)/shard_map/ppermute | solution.py:372
  90.9 4.5 %collective-permute-start.14 = (f32[4,4,8,128]{3,2,1,0:T(8,128)S(1)}, f32[4,4,8,128]{3,2,1,0:T(8,128)S(1)}, u32[]{:S(2)}, u32[]{:S(2)}) collective-permute-start(f32[4,4,8,128]{3,2,1,0:T(8,128)S(1)} %get-tuple-element.17), channel_id=1, source_target_pairs={{0,1},{1,0},{2,3},{3,2},{4,5},{5,4},{6,7},{7,6},{8,9},{9,8},{10,11... | collective-permute-start | bytes 196616 | tf_op jit(solution)/shard_map/ppermute | solution.py:373
  92.5 2.9 %collective-permute-start.13 = (f32[4,4,8,128]{3,2,1,0:T(8,128)S(1)}, f32[4,4,8,128]{3,2,1,0:T(8,128)S(1)}, u32[]{:S(2)}, u32[]{:S(2)}) collective-permute-start(f32[4,4,8,128]{3,2,1,0:T(8,128)S(1)} %get-tuple-element.16), channel_id=1, source_target_pairs={{0,2},{2,0},{4,6},{6,4},{8,10},{10,8},{12,14},{14,12},{16,18},{18,... | collective-permute-start | bytes 196616 | tf_op jit(solution)/shard_map/ppermute | solution.py:371
  92.7 4.4 %collective-permute-start.16 = (f32[4,4,8,128]{3,2,1,0:T(8,128)S(1)}, f32[4,4,8,128]{3,2,1,0:T(8,128)S(1)}, u32[]{:S(2)}, u32[]{:S(2)}) collective-permute-start(f32[4,4,8,128]{3,2,1,0:T(8,128)S(1)} %collective-permute-done.15), channel_id=1, source_target_pairs={{0,1},{1,0},{2,3},{3,2},{4,5},{5,4},{6,7},{7,6},{8,9},{9,8},{10,11... | collective-permute-start | bytes 196616 | tf_op jit(solution)/shard_map/ppermute | solution.py:374
